TPU v7x, 32 devices: a whole 2x2x4 slice. The times are simulated.
32 devices in a mesh: batch: 2 (over y), seq: 4 (over x, core), mp: 4 (over z).
Axes of the slice: x: 2, y: 2, z: 4, core: 2. Of those that a mesh axis runs over, the one named last changes fastest.
Arguments:
- tokens: bfloat16 [4096, 2048], P(('batch', 'seq')), may hold values from -6 to 6
- segment_ids: int32 [2, 2048], P('batch'), may hold values from 0 to 3, never falling along the last dimension, each value on 1 to 1024 neighbouring positions
- attn_gain: float32 [2048], replicated, may hold values from 0.5 to 1.5
- w_query: bfloat16 [2048, 2048], P(None, 'mp'), may hold values from -1 to 1
- w_key: bfloat16 [2048, 512], P(None, 'mp'), may hold values from -1 to 1
- w_value: bfloat16 [2048, 512], P(None, 'mp'), may hold values from -0.125 to 0.125
- w_output: bfloat16 [2048, 2048], P('mp'), may hold values from -1 to 1
- mlp_gain: float32 [2048], replicated, may hold values from 0.5 to 1.5
- w_gate: bfloat16 [2048, 8192], P(None, 'mp'), may hold values from -0.125 to 0.125
- w_up: bfloat16 [2048, 8192], P(None, 'mp'), may hold values from -0.125 to 0.125
- w_down: bfloat16 [8192, 2048], P('mp'), may hold values from -0.0625 to 0.0625
- cotangent: bfloat16 [4096, 2048], P(('batch', 'seq')), may hold values from -6 to 6
Outputs:
- output: bfloat16 [4096, 2048], P(('batch', 'seq'))
- grad_tokens: bfloat16 [4096, 2048], P(('batch', 'seq'))
- grad_attn_gain: float32 [2048], P(('batch', 'seq'))
- grad_query: float32 [2048, 2048], P(('batch', 'seq'), 'mp')
- grad_key: float32 [2048, 512], P(('batch', 'seq'), 'mp')
- grad_value: float32 [2048, 512], P(('batch', 'seq'), 'mp')
- grad_output: float32 [2048, 2048], P('mp', ('batch', 'seq'))
- grad_mlp_gain: float32 [2048], P(('batch', 'seq'))
- grad_gate: float32 [2048, 8192], P(('batch', 'seq'), 'mp')
- grad_up: float32 [2048, 8192], P(('batch', 'seq'), 'mp')
- grad_down: float32 [8192, 2048], P('mp', ('batch', 'seq'))
Inputs may be any that keep to these rules, and one draw needn't show every extreme that they name: `segment_ids`: within a row the ids never fall; a document (a run of one id) has 1 to 1024 tokens, and some document has exactly 1024.
All inputs are finite; a program needn't handle non-finite values.
Results may differ from a plain program's by a relative error of at most 0.025.
Values may be sent and summed in bfloat16 or wider, within the bound.
A program may use at most 256 MiB of HBM per device.

v0:
```python
import math
import jax
import jax.numpy as jnp
from jax import lax
from jax.sharding import PartitionSpec as P

HS = 64
rope_base = 500000.0
epsilon = 1e-05
masked_score = -1e30


def tables(seq_ids):
    positions = jnp.arange(seq_ids.shape[0], dtype=jnp.int32)
    before = jnp.concatenate([seq_ids[:1] - 1, seq_ids[:-1]])
    doc_start = lax.cummax(jnp.where(seq_ids != before, positions, 0), axis=0)
    doc_place = (positions - doc_start).astype(jnp.float32)
    half_width = HS // 2
    frequency = jnp.exp(
        jnp.arange(half_width, dtype=jnp.float32) * (-2.0 * math.log(rope_base) / HS)
    )
    angles = doc_place[:, None] * frequency[None, :]
    angles = jnp.concatenate([angles, angles], axis=1)
    return (jnp.cos(angles), jnp.sin(angles))


def rotate_half(values):
    half_width = values.shape[-1] // 2
    return jnp.concatenate([-values[..., half_width:], values[..., :half_width]], axis=-1)


def rope_apply(values, cos_table, sin_table):
    return values * cos_table + rotate_half(values) * sin_table


def rope_back(gradient, cos_table, sin_table):
    return gradient * cos_table - rotate_half(gradient * sin_table)


def product(left_side, right_side):
    return jnp.dot(left_side, right_side, preferred_element_type=jnp.float32)


def score_block(query_block, key_all, segments, first_row):
    score_scale = HS ** (-0.5)
    scores = (
        jnp.einsum("qgrd,kgd->grqk", query_block, key_all, preferred_element_type=jnp.float32)
        * score_scale
    )
    row_count = query_block.shape[0]
    row_index = first_row + jnp.arange(row_count, dtype=jnp.int32)
    key_index = jnp.arange(key_all.shape[0], dtype=jnp.int32)
    row_segment = lax.dynamic_slice_in_dim(segments, first_row, row_count, 0)
    allowed = (row_segment[:, None] == segments[None, :]) & (
        key_index[None, :] <= row_index[:, None]
    )
    return (scores, allowed)


def attend_forward(queries, key_all, value_all, segments, first_row):
    total_rows = queries.shape[0]
    block_rows = min(512, total_rows)

    def one_block(block_start):
        query_block = lax.dynamic_slice_in_dim(queries, block_start, block_rows, 0)
        scores, allowed = score_block(query_block, key_all, segments, first_row + block_start)
        scores = jnp.where(allowed[None, None], scores, masked_score)
        row_max = jnp.max(scores, axis=-1, keepdims=True)
        powers = jnp.exp(scores - row_max)
        totals = jnp.sum(powers, axis=-1, keepdims=True)
        shares = (powers / totals).astype(jnp.bfloat16)
        mixed_out = jnp.einsum(
            "grqk,kgd->qgrd", shares, value_all, preferred_element_type=jnp.float32
        )
        return (mixed_out.astype(jnp.bfloat16), (row_max + jnp.log(totals))[..., 0])

    starts = jnp.arange(total_rows // block_rows, dtype=jnp.int32) * block_rows
    mixed_out, log_total = lax.map(one_block, starts)
    return (mixed_out.reshape(queries.shape), log_total)


def attend_backward(
    queries, key_all, value_all, grad_mixed, log_total, segments, first_row, group_size
):
    total_rows, group_count, head_count, head_width = queries.shape
    copies = head_count // group_size
    block_rows = min(512, total_rows)
    seq_length = key_all.shape[0]
    score_scale = HS ** (-0.5)

    def one_block(carried, inputs):
        grad_key_acc, grad_value_acc = carried
        block_start, log_block = inputs
        query_block = lax.dynamic_slice_in_dim(queries, block_start, block_rows, 0)
        grad_block = lax.dynamic_slice_in_dim(grad_mixed, block_start, block_rows, 0)
        scores, allowed = score_block(query_block, key_all, segments, first_row + block_start)
        shares = jnp.where(allowed[None, None], jnp.exp(scores - log_block[..., None]), 0.0)
        shares_low = shares.astype(jnp.bfloat16)
        grad_split = grad_block.reshape(block_rows, group_count, copies, group_size, head_width)
        grad_value_acc = grad_value_acc + jnp.einsum(
            "gcjqk,qgcjd->kgcd",
            shares_low.reshape(group_count, copies, group_size, block_rows, seq_length),
            grad_split,
            preferred_element_type=jnp.float32,
        )
        grad_shares = jnp.einsum(
            "qgrd,kgd->grqk", grad_block, value_all, preferred_element_type=jnp.float32
        )
        grad_scores = shares * (grad_shares - jnp.sum(shares * grad_shares, axis=-1, keepdims=True))
        scores_low = grad_scores.astype(jnp.bfloat16)
        grad_query = (
            jnp.einsum("grqk,kgd->qgrd", scores_low, key_all, preferred_element_type=jnp.float32)
            * score_scale
        )
        grad_key_acc = (
            grad_key_acc
            + jnp.einsum(
                "gcjqk,qgcjd->kgcd",
                scores_low.reshape(group_count, copies, group_size, block_rows, seq_length),
                query_block.reshape(block_rows, group_count, copies, group_size, head_width),
                preferred_element_type=jnp.float32,
            )
            * score_scale
        )
        return ((grad_key_acc, grad_value_acc), grad_query)

    zero_state = jnp.zeros((seq_length, group_count, copies, head_width), jnp.float32)
    starts = jnp.arange(total_rows // block_rows, dtype=jnp.int32) * block_rows
    (grad_key_acc, grad_value_acc), grad_query = lax.scan(
        one_block, (zero_state, zero_state), (starts, log_total)
    )
    return (grad_query.reshape(queries.shape), grad_key_acc, grad_value_acc)


def local(
    tokens,
    segment_ids,
    attn_gain,
    w_query,
    w_key,
    w_value,
    w_output,
    mlp_gain,
    w_gate,
    w_up,
    w_down,
    cotangent,
):
    row_count = tokens.shape[0]
    seq_count = lax.axis_size("seq")
    seq_index = lax.axis_index("seq")
    segments = segment_ids[0]
    seq_length = segments.shape[0]
    first_row = seq_index * row_count
    cos_table, sin_table = tables(segments)
    cos_local = lax.dynamic_slice_in_dim(cos_table, first_row, row_count, 0)[:, None, :]
    sin_local = lax.dynamic_slice_in_dim(sin_table, first_row, row_count, 0)[:, None, :]
    heads_local = w_query.shape[1] // HS
    kv_local = w_key.shape[1] // HS
    group_size = heads_local // kv_local
    per_device = heads_local // seq_count
    copies = group_size // per_device
    inputs_wide = tokens.astype(jnp.float32)
    scale_one = lax.rsqrt(jnp.mean(inputs_wide * inputs_wide, axis=-1, keepdims=True) + epsilon)
    normed = (inputs_wide * scale_one * attn_gain).astype(jnp.bfloat16)
    query_rot = rope_apply(
        product(normed, w_query).reshape(row_count, heads_local, HS), cos_local, sin_local
    ).astype(jnp.bfloat16)
    key_rot = rope_apply(
        product(normed, w_key).reshape(row_count, kv_local, HS), cos_local, sin_local
    ).astype(jnp.bfloat16)
    value_low = product(normed, w_value).reshape(row_count, kv_local, HS).astype(jnp.bfloat16)
    key_slots = jnp.repeat(key_rot, copies, axis=1)
    value_slots = jnp.repeat(value_low, copies, axis=1)
    pair_slots = jnp.concatenate([key_slots, value_slots], axis=2)
    query_slots = query_rot.reshape(row_count, seq_count, per_device * HS)
    query_heads, pair_heads = (
        lax.all_to_all(query_slots, "seq", split_axis=1, concat_axis=0, tiled=True),
        lax.all_to_all(pair_slots, "seq", split_axis=1, concat_axis=0, tiled=True),
    )
    query_heads = query_heads.reshape(seq_length, 1, per_device, HS)
    key_heads = pair_heads[:, :, :HS]
    value_heads = pair_heads[:, :, HS:]
    mixed_heads, log_total = attend_forward(query_heads, key_heads, value_heads, segments, 0)
    mixed_back = lax.all_to_all(
        mixed_heads.reshape(seq_length, 1, per_device * HS),
        "seq",
        split_axis=0,
        concat_axis=1,
        tiled=True,
    )
    mixed_out = mixed_back.reshape(row_count, heads_local * HS)
    branch = lax.psum(product(mixed_out, w_output).astype(jnp.bfloat16), "mp").astype(jnp.float32)
    middle = inputs_wide + branch
    scale_two = lax.rsqrt(jnp.mean(middle * middle, axis=-1, keepdims=True) + epsilon)
    normed_two = (middle * scale_two * mlp_gain).astype(jnp.bfloat16)
    gate_pre = product(normed_two, w_gate)
    up_pre = product(normed_two, w_up)
    sigmoid_gate = jax.nn.sigmoid(gate_pre)
    swish_gate = gate_pre * sigmoid_gate
    active = (swish_gate * up_pre).astype(jnp.bfloat16)
    mlp_out = lax.psum(product(active, w_down).astype(jnp.bfloat16), "mp").astype(jnp.float32)
    output = (middle + mlp_out).astype(jnp.bfloat16)
    grad_down = jnp.einsum("tf,td->fd", active, cotangent, preferred_element_type=jnp.float32)
    grad_active = jnp.einsum("td,fd->tf", cotangent, w_down, preferred_element_type=jnp.float32)
    grad_gate_low = (
        grad_active * up_pre * sigmoid_gate * (1.0 + gate_pre * (1.0 - sigmoid_gate))
    ).astype(jnp.bfloat16)
    grad_up_low = (grad_active * swish_gate).astype(jnp.bfloat16)
    grad_gate_w = jnp.einsum(
        "td,tf->df", normed_two, grad_gate_low, preferred_element_type=jnp.float32
    )
    grad_up_w = jnp.einsum("td,tf->df", normed_two, grad_up_low, preferred_element_type=jnp.float32)
    grad_normed_two = lax.psum(
        (
            jnp.einsum("tf,df->td", grad_gate_low, w_gate, preferred_element_type=jnp.float32)
            + jnp.einsum("tf,df->td", grad_up_low, w_up, preferred_element_type=jnp.float32)
        ).astype(jnp.bfloat16),
        "mp",
    ).astype(jnp.float32)
    scaled_two = grad_normed_two * mlp_gain
    grad_middle = (
        cotangent.astype(jnp.float32)
        + scale_two * scaled_two
        - middle
        * (scale_two * scale_two * scale_two)
        * jnp.mean(middle * scaled_two, axis=-1, keepdims=True)
    )
    grad_mlp_gain = jnp.sum(grad_normed_two * middle * scale_two, axis=0)
    grad_branch = grad_middle.astype(jnp.bfloat16)
    grad_output_w = jnp.einsum(
        "tc,td->cd", mixed_out, grad_branch, preferred_element_type=jnp.float32
    )
    grad_mixed = jnp.einsum(
        "td,cd->tc", grad_branch, w_output, preferred_element_type=jnp.float32
    ).astype(jnp.bfloat16)
    grad_heads = lax.all_to_all(
        grad_mixed.reshape(row_count, seq_count, per_device * HS),
        "seq",
        split_axis=1,
        concat_axis=0,
        tiled=True,
    )
    grad_heads = grad_heads.reshape(seq_length, 1, per_device, HS)
    grad_query, grad_key_copy, grad_value_copy = attend_backward(
        query_heads, key_heads, value_heads, grad_heads, log_total, segments, 0, per_device
    )
    cos_wide = cos_table[:, None, None, :]
    sin_wide = sin_table[:, None, None, :]
    grad_query_low = rope_back(grad_query, cos_wide, sin_wide).astype(jnp.bfloat16)
    grad_key_low = rope_back(grad_key_copy, cos_wide, sin_wide).astype(jnp.bfloat16)
    grad_pair = jnp.concatenate(
        [grad_key_low, grad_value_copy.astype(jnp.bfloat16)], axis=3
    ).reshape(seq_length, 1, 2 * HS)
    grad_query_tok, grad_pair_tok = (
        lax.all_to_all(
            grad_query_low.reshape(seq_length, 1, per_device * HS),
            "seq",
            split_axis=0,
            concat_axis=1,
            tiled=True,
        ),
        lax.all_to_all(grad_pair, "seq", split_axis=0, concat_axis=1, tiled=True),
    )
    grad_query_pre = grad_query_tok.reshape(row_count, heads_local * HS)
    pair_summed = jnp.sum(
        grad_pair_tok.astype(jnp.float32).reshape(row_count, kv_local, copies, 2 * HS), axis=2
    )
    grad_key_pre = pair_summed[:, :, :HS].reshape(row_count, kv_local * HS).astype(jnp.bfloat16)
    grad_value_pre = pair_summed[:, :, HS:].reshape(row_count, kv_local * HS).astype(jnp.bfloat16)
    grad_query_w = jnp.einsum(
        "td,tc->dc", normed, grad_query_pre, preferred_element_type=jnp.float32
    )
    grad_key_w = jnp.einsum("td,tc->dc", normed, grad_key_pre, preferred_element_type=jnp.float32)
    grad_value_w = jnp.einsum(
        "td,tc->dc", normed, grad_value_pre, preferred_element_type=jnp.float32
    )
    grad_normed = lax.psum(
        (
            jnp.einsum("tc,dc->td", grad_query_pre, w_query, preferred_element_type=jnp.float32)
            + jnp.einsum("tc,dc->td", grad_key_pre, w_key, preferred_element_type=jnp.float32)
            + jnp.einsum("tc,dc->td", grad_value_pre, w_value, preferred_element_type=jnp.float32)
        ).astype(jnp.bfloat16),
        "mp",
    ).astype(jnp.float32)
    scaled_one = grad_normed * attn_gain
    grad_inputs = (
        grad_middle
        + scale_one * scaled_one
        - inputs_wide
        * (scale_one * scale_one * scale_one)
        * jnp.mean(inputs_wide * scaled_one, axis=-1, keepdims=True)
    )
    grad_attn_gain = jnp.sum(grad_normed * inputs_wide * scale_one, axis=0)
    grad_tokens = grad_inputs.astype(jnp.bfloat16)
    summed = (
        lax.psum_scatter(
            grad_attn_gain.astype(jnp.bfloat16), ("batch", "seq"), scatter_dimension=0, tiled=True
        ).astype(jnp.float32),
        lax.psum_scatter(
            grad_query_w.astype(jnp.bfloat16), ("batch", "seq"), scatter_dimension=0, tiled=True
        ).astype(jnp.float32),
        lax.psum_scatter(
            grad_key_w.astype(jnp.bfloat16), ("batch", "seq"), scatter_dimension=0, tiled=True
        ).astype(jnp.float32),
        lax.psum_scatter(
            grad_value_w.astype(jnp.bfloat16), ("batch", "seq"), scatter_dimension=0, tiled=True
        ).astype(jnp.float32),
        lax.psum_scatter(
            grad_output_w.astype(jnp.bfloat16), ("batch", "seq"), scatter_dimension=1, tiled=True
        ).astype(jnp.float32),
        lax.psum_scatter(
            grad_mlp_gain.astype(jnp.bfloat16), ("batch", "seq"), scatter_dimension=0, tiled=True
        ).astype(jnp.float32),
        lax.psum_scatter(
            grad_gate_w.astype(jnp.bfloat16), ("batch", "seq"), scatter_dimension=0, tiled=True
        ).astype(jnp.float32),
        lax.psum_scatter(
            grad_up_w.astype(jnp.bfloat16), ("batch", "seq"), scatter_dimension=0, tiled=True
        ).astype(jnp.float32),
        lax.psum_scatter(
            grad_down.astype(jnp.bfloat16), ("batch", "seq"), scatter_dimension=1, tiled=True
        ).astype(jnp.float32),
    )
    return (
        output,
        grad_tokens,
        summed[0],
        summed[1],
        summed[2],
        summed[3],
        summed[4],
        summed[5],
        summed[6],
        summed[7],
        summed[8],
    )


def solution(mesh):
    in_specs = (
        P(("batch", "seq"), None),
        P("batch", None),
        P(),
        P(None, "mp"),
        P(None, "mp"),
        P(None, "mp"),
        P("mp", None),
        P(),
        P(None, "mp"),
        P(None, "mp"),
        P("mp", None),
        P(("batch", "seq"), None),
    )
    out_specs = (
        P(("batch", "seq"), None),
        P(("batch", "seq"), None),
        P(("batch", "seq")),
        P(("batch", "seq"), "mp"),
        P(("batch", "seq"), "mp"),
        P(("batch", "seq"), "mp"),
        P("mp", ("batch", "seq")),
        P(("batch", "seq")),
        P(("batch", "seq"), "mp"),
        P(("batch", "seq"), "mp"),
        P("mp", ("batch", "seq")),
    )
    return jax.shard_map(local, mesh=mesh, in_specs=in_specs, out_specs=out_specs, check_vma=False)
```

profile of v0, /device:TPU:0, one launch (start us, length us, event | category | flops | bytes accessed | tf_op | source)
XLA Modules:
  0.0 1099.2 jit_solution(13125591783962021573)
XLA Ops:
  24.8 4.2 all-to-all-start.1
  29.1 3.6 fusion.105
  34.2 3.7 all-to-all-done.1
  37.9 4.1 all-to-all-start
  44.8 6.1 all-to-all-done
  54.6 49.3 %while.27 = (s32[]{:T(128)}, bf16[4,512,1,2,64]{1,4,3,2,0:T(8,128)(2,1)}, f32[4,1,2,512]{3,2,1,0:T(2,128)S(1)}, s32[4]{0:T(128)S(1)}, s32[2048]{0:T(1024)S(1)}, ...) while((s32[]{:T(128)}, ...), condition=%wide.region_6.7_spmd, body=%wide.region_3.6_spmd.sunk | while | flops 565247488 | bytes 30198452 | solution.py:78
  63.8 3.3 fusion.176
  88.3 3.3 fusion.176
  103.9 3.6 copy.107
  107.5 5.0 reshape.582
  113.0 13.4 %reduce.6 = bf16[2048,128]{1,0:T(8,128)(2,1)} reduce(bf16[2048,1,128]{2,1,0:T(2,128)(2,1)} %reshape.582, bf16[]{:T(256)} %broadcast.317), dimensions={1}, to_apply=%reshape.582.reduce_sub_computation | reduce | bytes 1048578 | tf_op jit(solution)/shard_map/reshape;reshape | solution.py:186
  128.3 13.4 %all_to_all.87 = bf16[4,2,32768]{2,1,0:T(2,128)(2,1)} all-to-all(bf16[4,2,32768]{2,1,0:T(2,128)(2,1)} %reshape.586), channel_id=1, replica_groups=mesh['batch'=2,'seq'=4,'mp'=4] {'seq'}, dimensions={0} | all-to-all | bytes 1048576 | tf_op jit(solution)/shard_map/all_to_all | solution.py:185
  141.7 3.5 reshape.587
  149.3 3.6 convolution_convert_fusion.6
  153.0 87.3 %all-reduce.8.cloned.1.call-done = bf16[512,2048]{1,0:T(8,128)(2,1)} async-done(((bf16[512,2048]{1,0:T(8,128)(2,1)}), bf16[512,2048]{1,0:T(8,128)(2,1)}) %all-reduce.8.cloned.1.call-update) | async-done | bytes 2097168 | tf_op jit(solution)/shard_map/psum | solution.py:193
  244.9 7.7 fusion.109
  252.7 6.0 fusion.110
  258.8 11.9 %multiply_convert_fusion = (bf16[512,2048]{1,0:T(8,128)(2,1)}, bf16[512,2048]{1,0:T(8,128)(2,1)}, bf16[512,2048]{1,0:T(8,128)(2,1)}) fusion(f32[512,2048]{1,0:T(8,128)S(1)} %fusion.109, f32[512,2048]{1,0:T(8,128)} %fusion.110, bf16[512,2048]{1,0:T(8,128)(2,1)S(1)} %copy-done.21, bf16[2048,2048]{1,0:T(8,128)(2,1)} %param.26), kind=kOutput, calls=%fused_computation.98 | convolution fusion | flops 4310695936 | bytes 25165824 | tf_op jit(solution)/shard_map/td,fd->tf/dot_general | solution.py:205
  270.7 7.8 fusion.111
  278.5 9.6 add_convert_fusion.1
  288.1 85.4 %all-reduce.10.cloned.1.call-done = bf16[512,2048]{1,0:T(8,128)(2,1)} async-done(((bf16[512,2048]{1,0:T(8,128)(2,1)}), bf16[512,2048]{1,0:T(8,128)(2,1)}) %all-reduce.10.cloned.1.call-update) | async-done | bytes 2097168 | tf_op jit(solution)/shard_map/psum | solution.py:214
  373.5 5.2 fusion.73
  385.8 3.5 all-to-all-start.3
  389.3 8.7 all-to-all-done.3
  398.8 124.7 %while.28 = (s32[]{:T(128)}, f32[2048,1,1,64]{0,3,2,1:T(8,128)S(1)}, f32[2048,1,1,64]{0,3,2,1:T(8,128)}, f32[4,512,1,2,64]{1,0,4,3,2:T(4,128)}, s32[4]{0:T(128)S...) while((s32[]{:T(128)}, ...), condition=%wide.region_14.15_spmd.clone, body=%wide.region_12.14_spmd.clone.sunk | while | flops 1377500672 | bytes 126400856 | solution.py:129
  414.0 6.1 dynamic_update_slice.20
  423.3 6.6 fusion.190
  445.2 6.1 dynamic_update_slice.20
  454.5 6.6 fusion.190
  476.4 6.1 dynamic_update_slice.20
  485.7 6.6 fusion.190
  507.6 6.1 dynamic_update_slice.20
  516.9 6.6 fusion.190
  530.1 12.0 %all_to_all.88 = bf16[4,2,32768]{2,1,0:T(2,128)(2,1)} all-to-all(bf16[4,2,32768]{2,1,0:T(2,128)(2,1)S(1)} %reshape.590), channel_id=1, replica_groups=mesh['batch'=2,'seq'=4,'mp'=4] {'seq'}, dimensions={0} | all-to-all | bytes 1048576 | tf_op jit(solution)/shard_map/all_to_all | solution.py:263
  550.7 5.1 convolution_convert_fusion.3
  564.9 11.9 %all_to_all.89 = bf16[4,2,32768]{2,1,0:T(2,128)(2,1)} all-to-all(bf16[4,2,32768]{2,1,0:T(2,128)(2,1)S(1)} %reshape.588), channel_id=1, replica_groups=mesh['batch'=2,'seq'=4,'mp'=4] {'seq'}, dimensions={0} | all-to-all | bytes 1048576 | tf_op jit(solution)/shard_map/all_to_all | solution.py:256
  584.2 9.9 convolution_convert_fusion.5
  599.2 10.0 convolution_convert_fusion.2
  609.5 10.0 convolution_convert_fusion.1
  619.6 10.0 convolution_convert_fusion
  634.5 29.0 %reduce-scatter.14.cloned.1.call-done = bf16[512,256]{1,0:T(8,128)(2,1)} async-done(((bf16[512,2048]{1,0:T(8,128)(2,1)}), bf16[512,256]{1,0:T(8,128)(2,1)}) %reduce-scatter.14.cloned.1.call-update) | async-done | bytes 262160 | tf_op jit(solution)/shard_map/reduce_scatter | solution.py:309
  665.4 42.5 %reduce-scatter.8.cloned.1.call-done = bf16[256,512]{1,0:T(8,128)(2,1)} async-done(((bf16[2048,512]{1,0:T(8,128)(2,1)}), bf16[256,512]{1,0:T(8,128)(2,1)}) %reduce-scatter.8.cloned.1.call-update) | async-done | bytes 262160 | tf_op jit(solution)/shard_map/reduce_scatter | solution.py:300
  709.6 156.2 %all-reduce.12.cloned.1.call-done = (bf16[512,2048]{1,0:T(8,128)(2,1)}, bf16[512,2048]{1,0:T(8,128)(2,1)}) async-done(((bf16[512,2048]{1,0:T(8,128)(2,1)}, bf16[512,2048]{1,0:T(8,128)(2,1)}), (bf16[512,2048]{1,0:T(8,128)(2,1)}, bf16[512,2048]{1,0:T(8,128)(2,1)})) %all-reduce.12.cloned.1.call-update) | async-done | bytes 4194320 | tf_op jit(solution)/shard_map/psum | solution.py:202
  869.0 13.7 %all-reduce.2 = (bf16[2048]{0:T(1024)(128)(2,1)S(1)}, bf16[2048]{0:T(1024)(128)(2,1)S(1)}) all-reduce(bf16[2048]{0:T(1024)(128)(2,1)S(1)} %get-tuple-element.211, bf16[2048]{0:T(1024)(128)(2,1)S(1)} %copy-done.32), channel_id=2, replica_groups=mesh['batch'=2,'seq'=4,'mp'=4] {'batch','seq'}, use_global_device_ids=true, to_apply=%region_19.20.clone | all-reduce | flops 4096 | bytes 16384
  884.0 7.3 fusion.68
  891.3 48.5 %reduce-scatter.16.cloned.1.call-done = bf16[256,2048]{1,0:T(8,128)(2,1)} async-done(((bf16[2048,2048]{1,0:T(8,128)(2,1)}), bf16[256,2048]{1,0:T(8,128)(2,1)}) %reduce-scatter.16.cloned.1.call-update) | async-done | bytes 1048592 | tf_op jit(solution)/shard_map/reduce_scatter | solution.py:315
  942.6 72.2 %reduce-scatter.18.cloned.1.call-done = bf16[256,2048]{1,0:T(8,128)(2,1)} async-done(((bf16[2048,2048]{1,0:T(8,128)(2,1)}), bf16[256,2048]{1,0:T(8,128)(2,1)}) %reduce-scatter.18.cloned.1.call-update) | async-done | bytes 1048592 | tf_op jit(solution)/shard_map/reduce_scatter | solution.py:318
  1017.6 71.8 %reduce-scatter.20.cloned.1.call-done = bf16[2048,256]{1,0:T(8,128)(2,1)} async-done(((bf16[2048,2048]{1,0:T(8,128)(2,1)}), bf16[2048,256]{1,0:T(8,128)(2,1)}) %reduce-scatter.20.cloned.1.call-update) | async-done | bytes 1048592 | tf_op jit(solution)/shard_map/reduce_scatter | solution.py:321
  (290 shorter events, 201.3 us)
Async XLA Ops:
  7.2 142.1 %copy-start = (bf16[512,2048]{1,0:T(8,128)(2,1)S(1)}, bf16[512,2048]{1,0:T(8,128)(2,1)}, u32[]{:S(2)}) copy-start(bf16[512,2048]{1,0:T(8,128)(2,1)} %param.22) | copy-start | bytes 6291460
  10.6 9.7 copy-start.4
  10.6 9.7 copy-start.25
  10.6 9.7 copy-start.28
  13.3 8.7 copy-start.15
  13.3 8.7 copy-start.17
  16.4 12.7 %copy-start.30 = (f32[512]{0:T(512)}, f32[512]{0:T(512)S(1)}, u32[]{:S(2)}) copy-start(f32[512]{0:T(512)S(1)} %get-tuple-element.285) | copy-start | bytes 6148
  24.8 13.1 %all-to-all-start.1 = ((bf16[512,4,128]{0,2,1:T(8,128)(2,1)}), bf16[512,4,128]{0,2,1:T(8,128)(2,1)S(1)}, u32[]{:S(2)}, u32[]{:S(2)}) async-start(bf16[512,4,128]{0,2,1:T(8,128)(2,1)} %pad_maximum_fusion.2), calls=%async_computation.1 | async-start | bytes 1048576 | tf_op jit(solution)/shard_map/all_to_all | solution.py:179
  34.2 20.4 %copy-start.22 = (s32[1,2048]{1,0:T(1,128)S(1)}, s32[1,2048]{1,0:T(1,128)}, u32[]{:S(2)}) copy-start(s32[1,2048]{1,0:T(1,128)} %param.17) | copy-start | bytes 24580
  37.9 13.0 %all-to-all-start = ((bf16[512,4,128]{0,2,1:T(8,128)(2,1)}), bf16[512,4,128]{0,2,1:T(8,128)(2,1)}, u32[]{:S(2)}, u32[]{:S(2)}) async-start(bf16[512,4,128]{0,2,1:T(8,128)(2,1)} %fusion.83), calls=%async_computation | async-start | bytes 1048576 | tf_op jit(solution)/shard_map/all_to_all | solution.py:178
  42.1 198.2 %all-reduce.8.cloned.1.call-start = ((), (), s32[]{:S(2)}) async-start(), calls=%async_computation.13 | async-start | bytes 4194304 | tf_op jit(solution)/shard_map/psum | solution.py:193
  152.9 90.5 %copy-start.27 = (f32[2048]{0:T(1024)S(1)}, f32[2048]{0:T(1024)}, u32[]{:S(2)}) copy-start(f32[2048]{0:T(1024)} %param.23) | copy-start | bytes 24580
  153.0 220.5 %all-reduce.10.cloned.1.call-start = ((), (), s32[]{:S(2)}) async-start(), calls=%async_computation.14 | async-start | bytes 4194304 | tf_op jit(solution)/shard_map/psum | solution.py:214
  240.3 3.5 copy-start.8
  243.8 8.9 slice-start
  244.9 7.8 copy-start.19
  244.9 7.8 slice-start.1
  252.7 6.1 copy-start.21
  270.7 7.8 copy-start.35
  373.5 5.2 copy-start.6
  373.5 5.2 copy-start.9
  373.5 5.2 copy-start.11
  385.8 12.3 %all-to-all-start.3 = ((bf16[512,4,128]{0,2,1:T(8,128)(2,1)}), bf16[512,4,128]{0,2,1:T(8,128)(2,1)S(1)}, u32[]{:S(2)}, u32[]{:S(2)}) async-start(bf16[512,4,128]{0,2,1:T(8,128)(2,1)} %bitcast.384), calls=%async_computation.3 | async-start | bytes 1048576 | tf_op jit(solution)/shard_map/all_to_all | solution.py:237
  389.3 242.3 %reduce-scatter.10.cloned.1.call-start = ((), (), s32[]{:S(2)}) async-start(), calls=%async_computation.16 | async-start | bytes 589824 | tf_op jit(solution)/shard_map/reduce_scatter | solution.py:303
  398.8 124.7 %copy-start.18 = (f32[2048,1,1,32]{0,3,2,1:T(8,128)S(1)}, f32[2048,1,1,32]{0,3,2,1:T(8,128)}, u32[]{:S(2)}) copy-start(f32[2048,1,1,32]{0,3,2,1:T(8,128)} %get-tuple-element.282) | copy-start | bytes 786436
  398.8 5.9 copy-start.13
  423.3 6.6 copy-start.14
  430.0 5.9 copy-start.13
  454.5 6.7 copy-start.14
  461.2 5.9 copy-start.13
  485.7 6.7 copy-start.14
  492.4 5.9 copy-start.13
  516.9 6.6 copy-start.14
  529.6 17.1 %copy-start.7 = (bf16[512,2048]{1,0:T(8,128)(2,1)S(1)}, bf16[512,2048]{1,0:T(8,128)(2,1)}, u32[]{:S(2)}) copy-start(bf16[512,2048]{1,0:T(8,128)(2,1)} %param.16) | copy-start | bytes 6291460
  529.7 17.1 %copy-start.29 = (f32[2048]{0:T(1024)S(1)}, f32[2048]{0:T(1024)}, u32[]{:S(2)}) copy-start(f32[2048]{0:T(1024)} %param.18) | copy-start | bytes 24580
  529.7 17.0 %copy-start.31 = (f32[512]{0:T(512)S(1)}, f32[512]{0:T(512)}, u32[]{:S(2)}) copy-start(f32[512]{0:T(512)} %copy-done.30) | copy-start | bytes 6148
  548.6 84.4 %reduce-scatter.12.cloned.1.call-start = ((), (), s32[]{:S(2)}) async-start(), calls=%async_computation.17 | async-start | bytes 589824 | tf_op jit(solution)/shard_map/reduce_scatter | solution.py:306
  550.7 5.3 copy-start.12
  550.7 112.9 %reduce-scatter.14.cloned.1.call-start = ((), (), s32[]{:S(2)}) async-start(), calls=%async_computation.18 | async-start | bytes 2359296 | tf_op jit(solution)/shard_map/reduce_scatter | solution.py:309
  555.9 152.0 %reduce-scatter.8.cloned.1.call-start = ((), (), s32[]{:S(2)}) async-start(), calls=%async_computation.15 | async-start | bytes 2359296 | tf_op jit(solution)/shard_map/reduce_scatter | solution.py:300
  583.9 281.9 %all-reduce.12.cloned.1.call-start = ((), (), s32[]{:S(2)}) async-start(), calls=%async_computation.22 | async-start | bytes 8388608 | tf_op jit(solution)/shard_map/psum | solution.py:202
  584.2 9.9 copy-start.24
  599.1 340.7 %reduce-scatter.16.cloned.1.call-start = ((), (), s32[]{:S(2)}) async-start(), calls=%async_computation.19 | async-start | bytes 9437184 | tf_op jit(solution)/shard_map/reduce_scatter | solution.py:315
  609.2 405.6 %reduce-scatter.18.cloned.1.call-start = ((), (), s32[]{:S(2)}) async-start(), calls=%async_computation.20 | async-start | bytes 9437184 | tf_op jit(solution)/shard_map/reduce_scatter | solution.py:318
  619.5 469.9 %reduce-scatter.20.cloned.1.call-start = ((), (), s32[]{:S(2)}) async-start(), calls=%async_computation.21 | async-start | bytes 9437184 | tf_op jit(solution)/shard_map/reduce_scatter | solution.py:321
  629.6 239.4 %copy-start.32 = (bf16[2048]{0:T(1024)(128)(2,1)S(1)}, bf16[2048]{0:T(1024)(128)(2,1)}, u32[]{:S(2)}) copy-start(bf16[2048]{0:T(1024)(128)(2,1)} %get-tuple-element.209) | copy-start | bytes 12292
  629.6 254.4 %copy-start.33 = (f32[512]{0:T(512)S(1)}, f32[512]{0:T(512)}, u32[]{:S(2)}) copy-start(f32[512]{0:T(512)} %get-tuple-element.284) | copy-start | bytes 6148
  884.0 208.1 %copy-start.1 = (bf16[512,2048]{1,0:T(8,128)(2,1)S(1)}, bf16[512,2048]{1,0:T(8,128)(2,1)}, u32[]{:S(2)}) copy-start(bf16[512,2048]{1,0:T(8,128)(2,1)} %param.22) | copy-start | bytes 6291460
  (15 other events, 31.9 us)
Sparse Core Ops, SparseCore 0:
  153.1 87.1 all-reduce.7
  288.2 85.1 all-reduce.9
  548.7 33.4 reduce-scatter.9
  585.2 34.0 reduce-scatter.11
  622.4 41.0 reduce-scatter.13
  666.7 41.0 reduce-scatter.7
  710.8 154.9 all-reduce.11
  869.3 70.4 reduce-scatter.15
  943.3 71.4 reduce-scatter.17
  1018.1 71.2 reduce-scatter.19
where the time goes:
time: 1110 us; the launch traced here: 1100 us
  waiting for transfers between devices  612 us (55%)
  matrix products  196 us (18%)
  other arithmetic  110 us (10%)
  local copies, waits for them, and re-layouts  85.5 us (8%)
  blocking collectives  51 us (5%)
  between operations  16.4 us (1%)
  loops' own time  16.2 us (1%)
  starting transfers between devices  12.7 us (1%)
    psum x1, waiting for transfers between devices, local(): lax.psum(product(active, w_down).astype(jnp.bfloat16), 'mp')  156 us
    psum x1, waiting for transfers between devices, local(): lax.psum(product(mixed_out, w_output).astype(jnp.bfloat16), 'mp')  87.3 us
    psum x1, waiting for transfers between devices, local(): lax.psum((jnp.einsum('tf,df->td', grad_gate_low, w_gate, preferred_elemen...  85.4 us
    reduce_scatter x1, waiting for transfers between devices, local(): lax.psum_scatter(grad_up_w.astype(jnp.bfloat16), ('batch', 'seq'), scatte...  72.2 us
    reduce_scatter x1, waiting for transfers between devices, local(): lax.psum_scatter(grad_down.astype(jnp.bfloat16), ('batch', 'seq'), scatte...  71.8 us
    reduce_scatter x1, waiting for transfers between devices, local(): lax.psum_scatter(grad_gate_w.astype(jnp.bfloat16), ('batch', 'seq'), scat...  48.5 us
    reduce_scatter x1, waiting for transfers between devices, local(): lax.psum_scatter(grad_query_w.astype(jnp.bfloat16), ('batch', 'seq'), sca...  42.5 us
    dot_general x7, matrix products, product(): return jnp.dot(left_side, right_side, preferred_element_type=jnp.float32)  35.1 us
  transfers between devices with their start and end apart: 13, of which 11 were waited for; matrix products, arithmetic and copies ran while one was open for 9% of the time, Pallas kernels for 0%

commit v1 on v0

--- a/solution.py
+++ b/solution.py
@@ -211,12 +211,15 @@
         "td,tf->df", normed_two, grad_gate_low, preferred_element_type=jnp.float32
     )
     grad_up_w = jnp.einsum("td,tf->df", normed_two, grad_up_low, preferred_element_type=jnp.float32)
-    grad_normed_two = lax.psum(
-        (
-            jnp.einsum("tf,df->td", grad_gate_low, w_gate, preferred_element_type=jnp.float32)
-            + jnp.einsum("tf,df->td", grad_up_low, w_up, preferred_element_type=jnp.float32)
-        ).astype(jnp.bfloat16),
-        "mp",
+    grad_normed_two = jnp.sum(
+        lax.all_gather(
+            (
+                jnp.einsum("tf,df->td", grad_gate_low, w_gate, preferred_element_type=jnp.float32)
+                + jnp.einsum("tf,df->td", grad_up_low, w_up, preferred_element_type=jnp.float32)
+            ).astype(jnp.bfloat16),
+            "mp",
+        ),
+        axis=0,
     ).astype(jnp.float32)
     scaled_two = grad_normed_two * mlp_gain
     grad_middle = (

time: 1110 us -> 1030 us (0.928)
  waiting for transfers between devices: 612 us -> 509 us
    all_gather x0 -> x1, waiting for transfers between devices: none -> 128 us  [local(): lax.all_gather((jnp.einsum('tf,df->td', grad_gate_low, w_gate, preferred_...]
    psum x1 -> x0, waiting for transfers between devices: 85.4 us -> none  [local(): lax.psum((jnp.einsum('tf,df->td', grad_gate_low, w_gate, preferred_elemen...]
    reduce_scatter x1, waiting for transfers between devices: 72.2 us -> 0.01 us  [local(): lax.psum_scatter(grad_up_w.astype(jnp.bfloat16), ('batch', 'seq'), scatte...]
    reduce_scatter x1, waiting for transfers between devices: 71.8 us -> 0.01 us  [local(): lax.psum_scatter(grad_down.astype(jnp.bfloat16), ('batch', 'seq'), scatte...]
    reduce_scatter x1, waiting for transfers between devices: 48.5 us -> 0.02 us  [local(): lax.psum_scatter(grad_gate_w.astype(jnp.bfloat16), ('batch', 'seq'), scat...]
    reduce_scatter x1, waiting for transfers between devices: 0.01 us -> 35.7 us  [local(): lax.psum_scatter(grad_value_w.astype(jnp.bfloat16), ('batch', 'seq'), sca...]
    reduce_scatter x1, waiting for transfers between devices: 29 us -> 42.9 us  [local(): lax.psum_scatter(grad_output_w.astype(jnp.bfloat16), ('batch', 'seq'), sc...]
  transfers between devices with their start and end apart: 13 -> 13, of which waited for: 11 -> 10; matrix products, arithmetic and copies ran while one was open for 9% -> 23% of each run, Pallas kernels for 0% -> 0%
where the time goes in v1:
time: 1030 us; the launch traced here: 1020 us
  waiting for transfers between devices  509 us (49%)
  matrix products  197 us (19%)
  other arithmetic  118 us (11%)
  local copies, waits for them, and re-layouts  86 us (8%)
  blocking collectives  61.6 us (6%)
  between operations  16.4 us (2%)
  loops' own time  16.2 us (2%)
  starting transfers between devices  13.1 us (1%)
    psum x1, waiting for transfers between devices, local(): lax.psum(product(active, w_down).astype(jnp.bfloat16), 'mp')  156 us
    all_gather x1, waiting for transfers between devices, local(): lax.all_gather((jnp.einsum('tf,df->td', grad_gate_low, w_gate, preferred_...  128 us
    psum x1, waiting for transfers between devices, local(): lax.psum(product(mixed_out, w_output).astype(jnp.bfloat16), 'mp')  87.2 us
    reduce_scatter x1, waiting for transfers between devices, local(): lax.psum_scatter(grad_output_w.astype(jnp.bfloat16), ('batch', 'seq'), sc...  42.9 us
    reduce_scatter x1, waiting for transfers between devices, local(): lax.psum_scatter(grad_query_w.astype(jnp.bfloat16), ('batch', 'seq'), sca...  42.6 us
    reduce_scatter x1, waiting for transfers between devices, local(): lax.psum_scatter(grad_value_w.astype(jnp.bfloat16), ('batch', 'seq'), sca...  35.7 us
    dot_general x7, matrix products, product(): return jnp.dot(left_side, right_side, preferred_element_type=jnp.float32)  34.2 us
    dot_general x4, matrix products, one_block(): jnp.einsum('gcjqk,qgcjd->kgcd', shares_low.reshape(group_count, copies, g...  27.7 us
  transfers between devices with their start and end apart: 13, of which 10 were waited for; matrix products, arithmetic and copies ran while one was open for 23% of the time, Pallas kernels for 0%

profile of v1, /device:TPU:0, one launch (start us, length us, event | category | flops | bytes accessed | tf_op | source)
XLA Modules:
  0.0 1017.3 jit_solution(16741404361178364633)
XLA Ops:
  24.9 4.2 all-to-all-start.1
  29.1 3.6 fusion.105
  34.2 3.7 all-to-all-done.1
  37.9 4.1 all-to-all-start
  44.8 6.1 all-to-all-done
  54.6 49.3 %while.27 = (s32[]{:T(128)}, bf16[4,512,1,2,64]{1,4,3,2,0:T(8,128)(2,1)}, f32[4,1,2,512]{3,2,1,0:T(2,128)S(1)}, s32[4]{0:T(128)S(1)}, s32[2048]{0:T(1024)S(1)}, ...) while((s32[]{:T(128)}, ...), condition=%wide.region_6.7_spmd, body=%wide.region_3.6_spmd.sunk | while | flops 565247488 | bytes 30198452 | solution.py:78
  63.8 3.3 fusion.176
  76.1 3.3 fusion.176
  88.3 3.3 fusion.176
  103.9 3.7 copy.107
  107.6 5.0 reshape.583
  113.1 13.4 %reduce.7 = bf16[2048,128]{1,0:T(8,128)(2,1)} reduce(bf16[2048,1,128]{2,1,0:T(2,128)(2,1)} %reshape.583, bf16[]{:T(256)} %broadcast.317), dimensions={1}, to_apply=%reshape.583.reduce_sub_computation | reduce | bytes 1048578 | tf_op jit(solution)/shard_map/reshape;reshape | solution.py:186
  128.4 13.4 %all_to_all.87 = bf16[4,2,32768]{2,1,0:T(2,128)(2,1)} all-to-all(bf16[4,2,32768]{2,1,0:T(2,128)(2,1)} %reshape.587), channel_id=1, replica_groups=mesh['batch'=2,'seq'=4,'mp'=4] {'seq'}, dimensions={0} | all-to-all | bytes 1048576 | tf_op jit(solution)/shard_map/all_to_all | solution.py:185
  141.8 3.5 reshape.588
  151.4 87.2 %all-reduce.7.cloned.1.call-done = bf16[512,2048]{1,0:T(8,128)(2,1)} async-done(((bf16[512,2048]{1,0:T(8,128)(2,1)}), bf16[512,2048]{1,0:T(8,128)(2,1)}) %all-reduce.7.cloned.1.call-update) | async-done | bytes 2097168 | tf_op jit(solution)/shard_map/psum | solution.py:193
  243.2 7.7 fusion.109
  251.0 6.1 fusion.110
  257.1 11.9 %multiply_convert_fusion = (bf16[512,2048]{1,0:T(8,128)(2,1)}, bf16[512,2048]{1,0:T(8,128)(2,1)}, bf16[512,2048]{1,0:T(8,128)(2,1)}) fusion(f32[512,2048]{1,0:T(8,128)S(1)} %fusion.109, f32[512,2048]{1,0:T(8,128)} %fusion.110, bf16[512,2048]{1,0:T(8,128)(2,1)S(1)} %copy-done.22, bf16[2048,2048]{1,0:T(8,128)(2,1)} %param.26), kind=kOutput, calls=%fused_computation.98 | convolution fusion | flops 4310695936 | bytes 25165824 | tf_op jit(solution)/shard_map/td,fd->tf/dot_general | solution.py:205
  269.1 7.8 fusion.111
  276.8 9.4 add_convert_fusion.1
  286.5 10.6 %convolution_convert_fusion.2 = bf16[2048,2048]{1,0:T(8,128)(2,1)} fusion(bf16[512,2048]{1,0:T(8,128)(2,1)} %copy-done.21, bf16[512,2048]{1,0:T(8,128)(2,1)} %get-tuple-element.264), kind=kOutput, calls=%fused_computation.74 | convolution fusion | flops 4299161600 | bytes 12582912 | tf_op jit(solution)/shard_map/td,tf->df/dot_general | solution.py:210
  297.1 10.4 %convolution_convert_fusion.1 = bf16[2048,2048]{1,0:T(8,128)(2,1)} fusion(bf16[512,2048]{1,0:T(8,128)(2,1)} %copy-done.21, bf16[512,2048]{1,0:T(8,128)(2,1)} %get-tuple-element.263), kind=kOutput, calls=%fused_computation.73 | convolution fusion | flops 4299161600 | bytes 12582912 | tf_op jit(solution)/shard_map/td,tf->df/dot_general | solution.py:213
  307.6 127.5 %all-gather.3.cloned.1.call-done = bf16[2048,2048]{1,0:T(8,128)(2,1)} async-done(((bf16[512,2048]{1,0:T(8,128)(2,1)}), bf16[2048,2048]{1,0:T(8,128)(2,1)}) %all-gather.3.cloned.1.call-update) | async-done | bytes 8388624 | tf_op jit(solution)/shard_map/all_gather | solution.py:215
  435.1 7.2 reduce_sum.95
  442.3 5.7 fusion.73
  456.1 3.5 all-to-all-start.3
  460.1 10.1 convolution_convert_fusion
  473.8 126.9 %while.28 = (s32[]{:T(128)}, f32[2048,1,1,64]{0,3,2,1:T(8,128)S(1)}, f32[2048,1,1,64]{0,3,2,1:T(8,128)}, f32[4,512,1,2,64]{1,0,4,3,2:T(4,128)}, s32[4]{0:T(128)S...) while((s32[]{:T(128)}, ...), condition=%wide.region_14.15_spmd.clone, body=%wide.region_12.14_spmd.clone.sunk | while | flops 1377500672 | bytes 126400856 | solution.py:129
  489.1 6.2 dynamic_update_slice.20
  498.4 6.7 fusion.190
  520.5 6.3 dynamic_update_slice.20
  526.7 3.7 fusion.189
  530.5 6.6 fusion.190
  552.4 6.2 dynamic_update_slice.20
  561.8 6.7 fusion.190
  583.8 6.1 dynamic_update_slice.20
  593.1 7.6 fusion.190
  607.2 16.6 %all_to_all.88 = bf16[4,2,32768]{2,1,0:T(2,128)(2,1)} all-to-all(bf16[4,2,32768]{2,1,0:T(2,128)(2,1)S(1)} %reshape.591), channel_id=1, replica_groups=mesh['batch'=2,'seq'=4,'mp'=4] {'seq'}, dimensions={0} | all-to-all | bytes 1048576 | tf_op jit(solution)/shard_map/all_to_all | solution.py:266
  632.4 5.0 convolution_convert_fusion.3
  646.4 18.0 %all_to_all.89 = bf16[4,2,32768]{2,1,0:T(2,128)(2,1)} all-to-all(bf16[4,2,32768]{2,1,0:T(2,128)(2,1)S(1)} %reshape.589), channel_id=1, replica_groups=mesh['batch'=2,'seq'=4,'mp'=4] {'seq'}, dimensions={0} | all-to-all | bytes 1048576 | tf_op jit(solution)/shard_map/all_to_all | solution.py:259
  671.8 10.0 convolution_convert_fusion.5
  697.0 4.0 reduce-scatter.10.cloned.1.call-done
  702.6 35.7 %reduce-scatter.12.cloned.1.call-done = bf16[256,128]{1,0:T(8,128)(2,1)} async-done(((bf16[2048,128]{1,0:T(8,128)(2,1)}), bf16[256,128]{1,0:T(8,128)(2,1)}) %reduce-scatter.12.cloned.1.call-update) | async-done | bytes 65552 | tf_op jit(solution)/shard_map/reduce_scatter | solution.py:309
  739.7 42.9 %reduce-scatter.14.cloned.1.call-done = bf16[512,256]{1,0:T(8,128)(2,1)} async-done(((bf16[512,2048]{1,0:T(8,128)(2,1)}), bf16[512,256]{1,0:T(8,128)(2,1)}) %reduce-scatter.14.cloned.1.call-update) | async-done | bytes 262160 | tf_op jit(solution)/shard_map/reduce_scatter | solution.py:312
  784.5 42.6 %reduce-scatter.8.cloned.1.call-done = bf16[256,512]{1,0:T(8,128)(2,1)} async-done(((bf16[2048,512]{1,0:T(8,128)(2,1)}), bf16[256,512]{1,0:T(8,128)(2,1)}) %reduce-scatter.8.cloned.1.call-update) | async-done | bytes 262160 | tf_op jit(solution)/shard_map/reduce_scatter | solution.py:303
  828.9 156.1 %all-reduce.9.cloned.1.call-done = (bf16[512,2048]{1,0:T(8,128)(2,1)}, bf16[512,2048]{1,0:T(8,128)(2,1)}) async-done(((bf16[512,2048]{1,0:T(8,128)(2,1)}, bf16[512,2048]{1,0:T(8,128)(2,1)}), (bf16[512,2048]{1,0:T(8,128)(2,1)}, bf16[512,2048]{1,0:T(8,128)(2,1)})) %all-reduce.9.cloned.1.call-update) | async-done | bytes 4194320 | tf_op jit(solution)/shard_map/psum | solution.py:202
  988.1 13.7 %all-reduce.2 = (bf16[2048]{0:T(1024)(128)(2,1)S(1)}, bf16[2048]{0:T(1024)(128)(2,1)S(1)}) all-reduce(bf16[2048]{0:T(1024)(128)(2,1)S(1)} %get-tuple-element.211, bf16[2048]{0:T(1024)(128)(2,1)S(1)} %copy-done.35), channel_id=3, replica_groups=mesh['batch'=2,'seq'=4,'mp'=4] {'batch','seq'}, use_global_device_ids=true, to_apply=%region_19.20.clone | all-reduce | flops 4096 | bytes 16384
  1003.2 7.1 fusion.68
  (297 shorter events, 201.1 us)
Async XLA Ops:
  7.2 141.5 %copy-start = (bf16[512,2048]{1,0:T(8,128)(2,1)S(1)}, bf16[512,2048]{1,0:T(8,128)(2,1)}, u32[]{:S(2)}) copy-start(bf16[512,2048]{1,0:T(8,128)(2,1)} %param.22) | copy-start | bytes 6291460
  10.6 9.7 copy-start.4
  10.6 9.7 copy-start.27
  10.6 9.7 copy-start.31
  13.3 8.6 copy-start.17
  13.3 8.6 copy-start.19
  16.4 12.7 %copy-start.33 = (f32[512]{0:T(512)}, f32[512]{0:T(512)S(1)}, u32[]{:S(2)}) copy-start(f32[512]{0:T(512)S(1)} %get-tuple-element.285) | copy-start | bytes 6148
  24.9 13.1 %all-to-all-start.1 = ((bf16[512,4,128]{0,2,1:T(8,128)(2,1)}), bf16[512,4,128]{0,2,1:T(8,128)(2,1)S(1)}, u32[]{:S(2)}, u32[]{:S(2)}) async-start(bf16[512,4,128]{0,2,1:T(8,128)(2,1)} %pad_maximum_fusion.2), calls=%async_computation.1 | async-start | bytes 1048576 | tf_op jit(solution)/shard_map/all_to_all | solution.py:179
  34.2 20.4 %copy-start.24 = (s32[1,2048]{1,0:T(1,128)S(1)}, s32[1,2048]{1,0:T(1,128)}, u32[]{:S(2)}) copy-start(s32[1,2048]{1,0:T(1,128)} %param.17) | copy-start | bytes 24580
  37.9 13.0 %all-to-all-start = ((bf16[512,4,128]{0,2,1:T(8,128)(2,1)}), bf16[512,4,128]{0,2,1:T(8,128)(2,1)}, u32[]{:S(2)}, u32[]{:S(2)}) async-start(bf16[512,4,128]{0,2,1:T(8,128)(2,1)} %fusion.83), calls=%async_computation | async-start | bytes 1048576 | tf_op jit(solution)/shard_map/all_to_all | solution.py:178
  42.1 196.5 %all-reduce.7.cloned.1.call-start = ((), (), s32[]{:S(2)}) async-start(), calls=%async_computation.13 | async-start | bytes 4194304 | tf_op jit(solution)/shard_map/psum | solution.py:193
  103.9 41.4 %copy-start.12 = (bf16[2048,1,2,64]{0,3,2,1:T(8,128)(2,1)}, bf16[2048,1,2,64]{0,3,2,1:T(8,128)(2,1)S(1)}, u32[]{:S(2)}) copy-start(bf16[2048,1,2,64]{0,3,2,1:T(8,128)(2,1)S(1)} %get-tuple-element.534) | copy-start | bytes 1572868
  148.7 93.0 %copy-start.29 = (bf16[512,4,1,128]{0,3,1,2:T(8,128)(2,1)}, bf16[512,4,1,128]{0,3,1,2:T(8,128)(2,1)S(1)}, u32[]{:S(2)}) copy-start(bf16[512,4,1,128]{0,3,1,2:T(8,128)(2,1)S(1)} %copy.94) | copy-start | bytes 1572868
  151.3 90.4 %copy-start.30 = (f32[2048]{0:T(1024)S(1)}, f32[2048]{0:T(1024)}, u32[]{:S(2)}) copy-start(f32[2048]{0:T(1024)} %param.23) | copy-start | bytes 24580
  151.3 283.8 %all-gather.3.cloned.1.call-start = ((), (), s32[]{:S(2)}) async-start(), calls=%async_computation.21 | async-start | bytes 10485760 | tf_op jit(solution)/shard_map/all_gather | solution.py:215
  242.0 8.9 slice-start
  243.2 7.8 copy-start.21
  243.2 7.8 slice-start.1
  251.0 6.1 copy-start.22
  269.1 7.8 copy-start.38
  286.3 402.4 %reduce-scatter.16.cloned.1.call-start = ((), (), s32[]{:S(2)}) async-start(), calls=%async_computation.18 | async-start | bytes 9437184 | tf_op jit(solution)/shard_map/reduce_scatter | solution.py:318
  297.1 394.4 %reduce-scatter.18.cloned.1.call-start = ((), (), s32[]{:S(2)}) async-start(), calls=%async_computation.19 | async-start | bytes 9437184 | tf_op jit(solution)/shard_map/reduce_scatter | solution.py:321
  442.3 5.7 copy-start.6
  442.3 5.7 copy-start.9
  442.3 6.4 copy-start.10
  456.1 16.9 %all-to-all-start.3 = ((bf16[512,4,128]{0,2,1:T(8,128)(2,1)}), bf16[512,4,128]{0,2,1:T(8,128)(2,1)S(1)}, u32[]{:S(2)}, u32[]{:S(2)}) async-start(bf16[512,4,128]{0,2,1:T(8,128)(2,1)} %bitcast.386), calls=%async_computation.3 | async-start | bytes 1048576 | tf_op jit(solution)/shard_map/all_to_all | solution.py:240
  459.6 234.7 %reduce-scatter.20.cloned.1.call-start = ((), (), s32[]{:S(2)}) async-start(), calls=%async_computation.20 | async-start | bytes 9437184 | tf_op jit(solution)/shard_map/reduce_scatter | solution.py:324
  470.1 230.9 %reduce-scatter.10.cloned.1.call-start = ((), (), s32[]{:S(2)}) async-start(), calls=%async_computation.15 | async-start | bytes 589824 | tf_op jit(solution)/shard_map/reduce_scatter | solution.py:306
  473.8 128.2 %copy-start.20 = (f32[2048,1,1,32]{0,3,2,1:T(8,128)S(1)}, f32[2048,1,1,32]{0,3,2,1:T(8,128)}, u32[]{:S(2)}) copy-start(f32[2048,1,1,32]{0,3,2,1:T(8,128)} %get-tuple-element.282) | copy-start | bytes 786436
  473.9 5.9 copy-start.15
  498.4 6.7 copy-start.16
  505.1 6.0 copy-start.15
  530.5 6.7 copy-start.16
  537.1 6.0 copy-start.15
  561.8 6.8 copy-start.16
  568.5 6.0 copy-start.15
  593.1 7.6 copy-start.16
  606.8 21.6 %copy-start.7 = (bf16[512,2048]{1,0:T(8,128)(2,1)S(1)}, bf16[512,2048]{1,0:T(8,128)(2,1)}, u32[]{:S(2)}) copy-start(bf16[512,2048]{1,0:T(8,128)(2,1)} %param.16) | copy-start | bytes 6291460
  606.8 21.6 %copy-start.32 = (f32[2048]{0:T(1024)S(1)}, f32[2048]{0:T(1024)}, u32[]{:S(2)}) copy-start(f32[2048]{0:T(1024)} %param.18) | copy-start | bytes 24580
  606.8 21.6 %copy-start.34 = (f32[512]{0:T(512)S(1)}, f32[512]{0:T(512)}, u32[]{:S(2)}) copy-start(f32[512]{0:T(512)} %copy-done.33) | copy-start | bytes 6148
  630.2 108.0 %reduce-scatter.12.cloned.1.call-start = ((), (), s32[]{:S(2)}) async-start(), calls=%async_computation.16 | async-start | bytes 589824 | tf_op jit(solution)/shard_map/reduce_scatter | solution.py:309
  632.3 150.4 %reduce-scatter.14.cloned.1.call-start = ((), (), s32[]{:S(2)}) async-start(), calls=%async_computation.17 | async-start | bytes 2359296 | tf_op jit(solution)/shard_map/reduce_scatter | solution.py:312
  637.4 189.7 %reduce-scatter.8.cloned.1.call-start = ((), (), s32[]{:S(2)}) async-start(), calls=%async_computation.14 | async-start | bytes 2359296 | tf_op jit(solution)/shard_map/reduce_scatter | solution.py:303
  671.6 10.2 %copy-start.26 = (bf16[2048,128]{1,0:T(8,128)(2,1)S(1)}, bf16[2048,128]{1,0:T(8,128)(2,1)}, u32[]{:S(2)}) copy-start(bf16[2048,128]{1,0:T(8,128)(2,1)} %param.20) | copy-start | bytes 1572868
  671.6 313.4 %all-reduce.9.cloned.1.call-start = ((), (), s32[]{:S(2)}) async-start(), calls=%async_computation.22 | async-start | bytes 8388608 | tf_op jit(solution)/shard_map/psum | solution.py:202
  694.3 293.8 %copy-start.35 = (bf16[2048]{0:T(1024)(128)(2,1)S(1)}, bf16[2048]{0:T(1024)(128)(2,1)}, u32[]{:S(2)}) copy-start(bf16[2048]{0:T(1024)(128)(2,1)} %get-tuple-element.209) | copy-start | bytes 12292
  694.3 308.8 %copy-start.36 = (f32[512]{0:T(512)S(1)}, f32[512]{0:T(512)}, u32[]{:S(2)}) copy-start(f32[512]{0:T(512)} %get-tuple-element.284) | copy-start | bytes 6148
  1003.1 7.1 copy-start.1
  (18 other events, 44.5 us)
Sparse Core Ops, SparseCore 0:
  151.4 87.0 all-reduce.6
  286.4 148.6 all-gather.2
  438.6 71.0 reduce-scatter.15
  513.0 71.6 reduce-scatter.17
  587.9 78.1 reduce-scatter.19
  669.6 31.3 reduce-scatter.9
  704.1 34.0 reduce-scatter.11
  741.5 41.1 reduce-scatter.13
  786.0 41.0 reduce-scatter.7
  829.9 155.0 all-reduce.8
